TPU v7x, 32 devices: a 4x4x1 block of a 4x4x8 slice. The times are simulated.
32 devices in a mesh: dp: 1 (over z), ep2: 4 (over y), ep: 8 (over x, core).
Axes of the slice: x: 4, y: 4, z: 1, core: 2. Of those that a mesh axis runs over, the one named last changes fastest.
The devices are a block of a 4x4x8 slice.
Arguments:
- tokens: bfloat16 [4096, 2048], P(('dp', 'ep2', 'ep'))
- expert_idx: int32 [4096, 4], P(('dp', 'ep2', 'ep'))
- gates: float32 [4096, 4], P(('dp', 'ep2', 'ep'))
- w_gate: bfloat16 [32, 2048, 1792], P(('ep2', 'ep'))
- w_up: bfloat16 [32, 2048, 1792], P(('ep2', 'ep'))
- w_down: bfloat16 [32, 1792, 2048], P(('ep2', 'ep'))
Outputs:
- output: bfloat16 [4096, 2048], P(('dp', 'ep2', 'ep'))
All inputs are finite; a program needn't handle non-finite values.
Results may differ from a plain program's by a relative error of at most 0.00107.
Values are sent between devices in bfloat16 or wider.
A program may use at most 768 MiB of HBM per device.

v0:
```python
import jax
import jax.numpy as jnp
from jax import lax
from jax.sharding import PartitionSpec as P


def solution(mesh):
    n_outer = mesh.shape['ep2']
    n_inner = mesh.shape['ep']
    row_spec = P(('dp', 'ep2', 'ep'), None)
    weight_spec = P(('ep2', 'ep'), None, None)

    def local_step(tokens, expert_idx, gates, w_gate, w_up, w_down):
        tok_rows, d_model = tokens.shape
        top_k = expert_idx.shape[1]
        local_exp = w_gate.shape[0]
        n_experts = local_exp * n_outer * n_inner
        capacity = (tok_rows * top_k + n_experts - 1) // n_experts
        n_slots = n_experts * capacity
        flat_ids = expert_idx.reshape(-1)
        one_hot = (flat_ids[:, None] == jnp.arange(n_experts, dtype=jnp.int32)[None, :]).astype(jnp.int32)
        slot_rank = jnp.sum((jnp.cumsum(one_hot, axis=0) - 1) * one_hot, axis=1)
        slot_ids = flat_ids * capacity + slot_rank
        token_of = jnp.arange(tok_rows * top_k, dtype=jnp.int32) // top_k
        source_row = jax.ops.segment_sum(token_of - tok_rows, slot_ids, num_segments=n_slots) + tok_rows
        send_buf = jnp.take(tokens, source_row, axis=0, mode='fill', fill_value=0)
        send_buf = send_buf.reshape(n_outer, n_inner, local_exp, capacity, d_model)
        received = lax.all_to_all(send_buf, 'ep', 1, 1, tiled=True)
        received = lax.all_to_all(received, 'ep2', 0, 0, tiled=True)
        act_gate = jnp.einsum('abecd,edf->abecf', received, w_gate, preferred_element_type=jnp.float32)
        act_up = jnp.einsum('abecd,edf->abecf', received, w_up, preferred_element_type=jnp.float32)
        inner_act = (jax.nn.silu(act_gate) * act_up).astype(jnp.bfloat16)
        expert_out = jnp.einsum('abecf,efd->abecd', inner_act, w_down, preferred_element_type=jnp.float32).astype(jnp.bfloat16)
        returned = lax.all_to_all(expert_out, 'ep2', 0, 0, tiled=True)
        returned = lax.all_to_all(returned, 'ep', 1, 1, tiled=True)
        routed = jnp.take(returned.reshape(n_slots, d_model), slot_ids, axis=0).reshape(tok_rows, top_k, d_model)
        mixed = jnp.sum(gates[:, :, None] * routed, axis=1)
        return (tokens + mixed).astype(jnp.bfloat16)

    return jax.shard_map(local_step, mesh=mesh, in_specs=(row_spec, row_spec, row_spec, weight_spec, weight_spec, weight_spec), out_specs=row_spec, check_vma=False)
```

profile of v0, /device:TPU:97, one launch (start us, length us, event | category | flops | bytes accessed | tf_op | source)
XLA Modules:
  0.0 160.4 jit_solution(10827506386863295102)
XLA Ops:
  0.0 0.8 copy.36
  1.1 0.7 broadcast_multiply_fusion
  1.8 1.2 reduce-window.6
  2.9 0.2 slice_reduce_fusion
  3.5 4.1 %scatter_custom_fusion = s32[512]{0:T(512)S(1)} fusion(s32[512]{0:T(512)S(1)} %bitcast.98, s32[512]{0:T(512)S(1)} %fusion.26, s32[]{:T(128)} %constant.56.clone.1), kind=kCustom, calls=%fused_computation.47 | custom fusion | flops 512 | bytes 2052 | tf_op jit(solution)/shard_map/scatter-add | solution.py:25
  7.8 2.5 %gather_fusion = bf16[512,2048]{1,0:T(8,128)(2,1)S(1)} fusion(bf16[128,2048]{1,0:T(8,128)(2,1)S(1)} %copy-done, s32[1024]{0:T(1024)S(1)} %pad_clamp_fusion.1), kind=kCustom, calls=%fused_computation | custom fusion | bytes 4196352 | tf_op jit(solution)/shard_map/jit(_take)/gather | solution.py:26
  10.3 0.2 copy_select_fusion
  10.5 32.2 %all_to_all.20 = bf16[4,8,1,16,2048]{4,3,0,2,1:T(8,128)(2,1)S(1)} all-to-all(bf16[4,8,1,16,2048]{4,3,0,2,1:T(8,128)(2,1)S(1)} %copy_select_fusion), channel_id=1, replica_groups=mesh['dp'=1,'ep2'=4,'ep'=8] {'ep'}, dimensions={1} | all-to-all | bytes 4194304 | tf_op jit(solution)/shard_map/all_to_all | solution.py:28
  42.7 0.1 copy.44
  42.9 30.5 %all_to_all.21 = bf16[4,8,1,16,2048]{4,3,1,2,0:T(8,128)(2,1)S(1)} all-to-all(bf16[4,8,1,16,2048]{4,3,1,2,0:T(8,128)(2,1)S(1)} %copy.44), channel_id=1, replica_groups=mesh['dp'=1,'ep2'=4,'ep'=8] {'ep2'}, dimensions={0} | all-to-all | bytes 4194304 | tf_op jit(solution)/shard_map/all_to_all | solution.py:29
  73.4 4.0 %fusion.4 = f32[4,8,16,1792]{3,2,1,0:T(8,128)S(1)} fusion(bf16[1,2048,1792]{2,1,0:T(8,128)(2,1)S(1)} %bitcast.100, bf16[4,8,1,16,2048]{4,3,1,2,0:T(8,128)(2,1)S(1)} %all_to_all.21), kind=kOutput, calls=%fused_computation.7 | convolution fusion | flops 3758096384 | bytes 13107200 | tf_op jit(solution)/shard_map/abecd,edf->abecf/dot_general | solution.py:30
  77.4 4.2 %fusion.18 = bf16[4,8,16,1792]{3,2,1,0:T(8,128)(2,1)S(1)} fusion(bf16[1,2048,1792]{2,1,0:T(8,128)(2,1)S(1)} %bitcast.102, f32[4,8,16,1792]{3,2,1,0:T(8,128)S(1)} %fusion.4, bf16[4,8,1,16,2048]{4,3,1,2,0:T(8,128)(2,1)S(1)} %all_to_all.21), kind=kOutput, calls=%fused_computation.19 | convolution fusion | flops 3763601408 | bytes 14942208 | tf_op jit(solution)/shard_map/abecd,edf->abecf/dot_general | solution.py:31
  81.6 4.2 %fusion.15 = bf16[4,8,1,16,2048]{4,3,1,2,0:T(8,128)(2,1)S(1)} fusion(bf16[4,8,16,1792]{3,2,1,0:T(8,128)(2,1)S(1)} %fusion.18, bf16[1,1792,2048]{2,1,0:T(8,128)(2,1)S(1)} %bitcast.104), kind=kOutput, calls=%fused_computation.18 | convolution fusion | flops 3759144960 | bytes 11272192 | tf_op jit(solution)/shard_map/abecf,efd->abecd/dot_general | solution.py:33
  85.8 26.4 %all_to_all.22 = bf16[4,8,1,16,2048]{4,3,1,2,0:T(8,128)(2,1)S(1)} all-to-all(bf16[4,8,1,16,2048]{4,3,1,2,0:T(8,128)(2,1)S(1)} %fusion.15), channel_id=1, replica_groups=mesh['dp'=1,'ep2'=4,'ep'=8] {'ep2'}, dimensions={0} | all-to-all | bytes 4194304 | tf_op jit(solution)/shard_map/all_to_all | solution.py:34
  112.1 1.4 copy.46
  113.6 7.8 %all-to-all-start.3 = ((bf16[4,8,1,16,2048]{4,3,0,2,1:T(8,128)(2,1)}), bf16[4,8,1,16,2048]{4,3,0,2,1:T(8,128)(2,1)}, u32[]{:S(2)}, u32[]{:S(2)}) async-start(bf16[4,8,1,16,2048]{4,3,0,2,1:T(8,128)(2,1)} %copy.46), calls=%async_computation.3 | async-start | bytes 4194304 | tf_op jit(solution)/shard_map/all_to_all | solution.py:35
  121.6 0.1 copy.40
  121.8 0.1 copy.35
  121.9 25.7 %all-to-all-done.3 = bf16[4,8,1,16,2048]{4,3,0,2,1:T(8,128)(2,1)} async-done(((bf16[4,8,1,16,2048]{4,3,0,2,1:T(8,128)(2,1)}), bf16[4,8,1,16,2048]{4,3,0,2,1:T(8,128)(2,1)}, u32[]{:S(2)}, u32[]{:S(2)}) %all-to-all-start.3) | async-done | bytes 2097184 | tf_op jit(solution)/shard_map/all_to_all | solution.py:35
  147.6 1.7 %copy.47 = bf16[4,8,1,16,2048]{4,3,1,0,2:T(8,128)(2,1)S(1)} copy(bf16[4,8,1,16,2048]{4,3,0,2,1:T(8,128)(2,1)} %all-to-all-done.3) | data formatting | bytes 4194304 | tf_op jit(solution)/shard_map/all_to_all | solution.py:35
  149.3 3.3 %gather_fusion.1 = bf16[512,2048]{1,0:T(8,128)(2,1)} fusion(bf16[512,2048]{1,0:T(8,128)(2,1)S(1)} %bitcast.94, s32[1024]{0:T(1024)S(1)} %pad_clamp_fusion), kind=kCustom, calls=%fused_computation.1 | custom fusion | bytes 4196352 | tf_op jit(solution)/shard_map/jit(_take)/gather | solution.py:36
  152.7 2.7 %gather.15 = bf16[128,4,2048]{2,1,0:T(4,128)(2,1)S(1)} reshape(bf16[512,2048]{1,0:T(8,128)(2,1)} %gather_fusion.1) | data formatting | bytes 4194304 | tf_op jit(solution)/shard_map/jit(_take)/gather | solution.py:36
  155.4 4.1 %multiply_reduce_fusion = f32[128,2048]{1,0:T(8,128)S(1)} fusion(bf16[128,4,2048]{2,1,0:T(4,128)(2,1)S(1)} %gather.15, f32[128,4]{1,0:T(8,128)S(1)} %copy.35, pred[128,4]{1,0:T(8,128)(4,1)S(1)} %copy.40), kind=kLoop, calls=%fused_computation.9 | loop fusion | flops 3932160 | bytes 3148288 | tf_op jit(solution)/shard_map/reduce_sum | solution.py:37
  159.5 0.9 add_convert_fusion
  (40 shorter events, 1.0 us)
Async XLA Ops:
  0.0 7.8 %copy-start = (bf16[128,2048]{1,0:T(8,128)(2,1)S(1)}, bf16[128,2048]{1,0:T(8,128)(2,1)}, u32[]{:S(2)}) copy-start(bf16[128,2048]{1,0:T(8,128)(2,1)} %param.6) | copy-start | bytes 1572868
  10.3 63.1 %slice-start = ((s8[7340032]{0:T(1024)(128)(4,1)}), s8[4194304]{0:T(1024)(128)(4,1)S(1)}, s32[]{:S(2)}) async-start(s8[7340032]{0:T(1024)(128)(4,1)} %bitcast.99), calls=%async_computation.4 | async-start | bytes 8388608
  10.5 62.9 %slice-start.1 = ((s8[7340032]{0:T(1024)(128)(4,1)}), s8[3145728]{0:T(1024)(128)(4,1)S(1)}, s32[]{:S(2)}) async-start(s8[7340032]{0:T(1024)(128)(4,1)} %bitcast.99), calls=%async_computation.5 | async-start | bytes 6291456
  42.9 34.5 %slice-start.2 = ((s8[7340032]{0:T(1024)(128)(4,1)}), s8[4194304]{0:T(1024)(128)(4,1)S(1)}, s32[]{:S(2)}) async-start(s8[7340032]{0:T(1024)(128)(4,1)} %bitcast.101), calls=%async_computation.6 | async-start | bytes 8388608
  73.4 4.0 %slice-start.3 = ((s8[7340032]{0:T(1024)(128)(4,1)}), s8[3145728]{0:T(1024)(128)(4,1)S(1)}, s32[]{:S(2)}) async-start(s8[7340032]{0:T(1024)(128)(4,1)} %bitcast.101), calls=%async_computation.7 | async-start | bytes 6291456
  73.4 8.2 %slice-start.4 = ((s8[7340032]{0:T(1024)(128)(4,1)}), s8[4194304]{0:T(1024)(128)(4,1)S(1)}, s32[]{:S(2)}) async-start(s8[7340032]{0:T(1024)(128)(4,1)} %bitcast.103), calls=%async_computation.8 | async-start | bytes 8388608
  77.4 4.2 %slice-start.5 = ((s8[7340032]{0:T(1024)(128)(4,1)}), s8[3145728]{0:T(1024)(128)(4,1)S(1)}, s32[]{:S(2)}) async-start(s8[7340032]{0:T(1024)(128)(4,1)} %bitcast.103), calls=%async_computation.9 | async-start | bytes 6291456
  113.6 8.0 %copy-start.1 = (s32[128,4]{0,1:T(4,128)S(1)}, s32[128,4]{0,1:T(4,128)}, u32[]{:S(2)}) copy-start(s32[128,4]{0,1:T(4,128)} %param.7) | copy-start | bytes 6148
  113.6 8.2 %copy-start.2 = (f32[128,4]{0,1:T(4,128)S(1)}, f32[128,4]{0,1:T(4,128)}, u32[]{:S(2)}) copy-start(f32[128,4]{0,1:T(4,128)} %param.8) | copy-start | bytes 6148
  113.6 34.0 %all-to-all-start.3 = ((bf16[4,8,1,16,2048]{4,3,0,2,1:T(8,128)(2,1)}), bf16[4,8,1,16,2048]{4,3,0,2,1:T(8,128)(2,1)}, u32[]{:S(2)}, u32[]{:S(2)}) async-start(bf16[4,8,1,16,2048]{4,3,0,2,1:T(8,128)(2,1)} %copy.46), calls=%async_computation.3 | async-start | bytes 4194304 | tf_op jit(solution)/shard_map/all_to_all | solution.py:35
where the time goes:
time: 161 us; the launch traced here: 160 us
  blocking collectives  89.1 us (55%)
  waiting for transfers between devices  25.7 us (16%)
  local copies, waits for them, and re-layouts  13.9 us (9%)
  matrix products  12.3 us (8%)
  other arithmetic  11.4 us (7%)
  starting transfers between devices  7.82 us (5%)
    all_to_all x1, blocking collectives, local_step(): received = lax.all_to_all(send_buf, 'ep', 1, 1, tiled=True)  32.2 us
    all_to_all x1, blocking collectives, local_step(): received = lax.all_to_all(received, 'ep2', 0, 0, tiled=True)  30.5 us
    all_to_all x1, blocking collectives, local_step(): returned = lax.all_to_all(expert_out, 'ep2', 0, 0, tiled=True)  26.4 us
    all_to_all x1, waiting for transfers between devices, local_step(): returned = lax.all_to_all(returned, 'ep', 1, 1, tiled=True)  25.7 us
    all_to_all x1, starting transfers between devices, local_step(): returned = lax.all_to_all(returned, 'ep', 1, 1, tiled=True)  7.82 us
    gather x2, local copies, waits for them, and re-layouts, local_step(): jnp.take(returned.reshape(n_slots, d_model), slot_ids, axis=0)  6.08 us
    dot_general x1, matrix products, local_step(): jnp.einsum('abecd,edf->abecf', received, w_up, preferred_element_type=jnp...  4.17 us
    dot_general x1, matrix products, local_step(): jnp.einsum('abecf,efd->abecd', inner_act, w_down, preferred_element_type=...  4.16 us
  transfers between devices with their start and end apart: 1, of which 1 were waited for; matrix products, arithmetic and copies ran while one was open for 0% of the time, Pallas kernels for 0%

commit v1 on v0

v1 whole, which is shorter than its diff:
```python
import functools

import jax
import jax.numpy as jnp
from jax import lax
from jax.experimental import pallas as pl
from jax.experimental.pallas import tpu as pltpu
from jax.sharding import PartitionSpec as P

MESH = pl.DeviceIdType.MESH
BF16, F32, I32 = jnp.bfloat16, jnp.float32, jnp.int32
N_GROUPS = 4


def offsets_in_order(n_outer, n_inner):
    chips = n_inner // 2
    all_offsets = [(dy, dx, dc) for dc in (0, 1) for dy in range(n_outer) for dx in range(chips)]

    def hops(o):
        dy, dx, dc = o
        return min(dy, n_outer - dy) + min(dx, chips - dx)

    own = (0, 0, 0)
    far = sorted((o for o in all_offsets if o != own), key=lambda o: -hops(o))
    return [own] + far


def layer_kernel(order, n_outer, n_inner, idx_hbm, gate_hbm, tok_hbm, wg_hbm, wu_hbm, wd_hbm, out_ref,
                 idx_ref, gts_ref, tok_ref, wg_ref, wu_ref, wd_ref, slot_ref, sel_ref, perm_ref, gcol_ref,
                 send_ref, recv_ref, h_ref, y_ref, ret_ref,
                 in_sem, w_sem, out_send, out_recv, back_send, back_recv):
    dp, outer, inner = lax.axis_index('dp'), lax.axis_index('ep2'), lax.axis_index('ep')
    chips = n_inner // 2
    chip, core = inner // 2, inner % 2
    n_dev = n_outer * n_inner
    rows, d_model = tok_ref.shape
    top_k = idx_ref.shape[0]
    cap = (rows * top_k) // n_dev
    d_ff = wg_ref.shape[1]
    n_slots = n_dev * cap
    per_group = n_dev // N_GROUPS
    g_rows = n_slots // N_GROUPS

    def peer(o, sign):
        dy, dx, dc = o
        y = lax.rem(outer + (dy if sign > 0 else n_outer - dy), n_outer)
        x = lax.rem(chip + (dx if sign > 0 else chips - dx), chips)
        c = lax.rem(core + dc, 2)
        return y, x * 2 + c

    barrier = pltpu.get_barrier_semaphore()
    for o in order[1:]:
        y, x = peer(o, 1)
        pl.semaphore_signal(barrier, inc=1, device_id=(dp, y, x), device_id_type=MESH)

    idx_copy = pltpu.make_async_copy(idx_hbm, idx_ref, in_sem.at[0])
    tok_copy = pltpu.make_async_copy(tok_hbm, tok_ref, in_sem.at[1])
    gts_copy = pltpu.make_async_copy(gate_hbm, gts_ref, in_sem.at[2])
    w_copies = [pltpu.make_async_copy(h.at[0], v, w_sem.at[i])
                for i, (h, v) in enumerate(((wg_hbm, wg_ref), (wu_hbm, wu_ref), (wd_hbm, wd_ref)))]
    for copy in (idx_copy, tok_copy, gts_copy, *w_copies):
        copy.start()

    idx_copy.wait()
    expert = lax.broadcasted_iota(I32, (n_dev, rows), 0)
    chosen = jnp.zeros((n_dev, rows), F32)
    for j in range(top_k):
        chosen = chosen + jnp.where(idx_ref[j:j + 1, :] == expert, 1.0, 0.0)
    earlier = lax.broadcasted_iota(I32, (rows, rows), 0) < lax.broadcasted_iota(I32, (rows, rows), 1)
    rank = jnp.dot(chosen.astype(BF16), jnp.where(earlier, 1.0, 0.0).astype(BF16), preferred_element_type=F32)
    slot_ref[...] = jnp.where(chosen > 0.5, rank, -1.0)
    place = lax.broadcasted_iota(I32, (cap, rows), 0).astype(F32)
    for q, o in enumerate(order):
        y, x = peer(o, 1)
        row = slot_ref[pl.ds(y * n_inner + x, 1), :]
        sel_ref[q * cap:(q + 1) * cap, :] = jnp.where(row == place, 1.0, 0.0).astype(BF16)

    tok_copy.wait()
    for g in range(N_GROUPS):
        block = sel_ref[g * g_rows:(g + 1) * g_rows, :]
        send_ref[g * g_rows:(g + 1) * g_rows, :] = jnp.dot(block, tok_ref[...], preferred_element_type=F32).astype(BF16)
    pl.semaphore_wait(barrier, n_dev - 1)

    def copy_out(q):
        y, x = peer(order[q], 1)
        part = pl.ds(q * cap, cap)
        return pltpu.make_async_remote_copy(send_ref.at[part], recv_ref.at[part], out_send.at[q], out_recv.at[q],
                                            device_id=(dp, y, x), device_id_type=MESH)

    def copy_back(q):
        y, x = peer(order[q], -1)
        part = pl.ds(q * cap, cap)
        return pltpu.make_async_remote_copy(y_ref.at[part], ret_ref.at[part], back_send.at[q], back_recv.at[q],
                                            device_id=(dp, y, x), device_id_type=MESH)

    for q in range(1, n_dev):
        copy_out(q).start()
    recv_ref[0:cap, :] = send_ref[0:cap, :]

    gts_copy.wait()
    gcol_ref[...] = jnp.transpose(jnp.concatenate([gts_ref[...], jnp.zeros((8 - top_k, rows), F32)], axis=0))
    for g in range(N_GROUPS):
        for j in range(top_k):
            parts = []
            for q in range(g * per_group, (g + 1) * per_group):
                y, x = peer(order[q], 1)
                mine = jnp.where(idx_ref[j:j + 1, :] == y * n_inner + x, 1.0, 0.0)
                parts.append(sel_ref[q * cap:(q + 1) * cap, :].astype(F32) * mine)
            perm_ref[j * rows:(j + 1) * rows, g * g_rows:(g + 1) * g_rows] = jnp.transpose(
                jnp.concatenate(parts, axis=0)).astype(BF16)

    for g in range(N_GROUPS):
        for q in range(g * per_group, (g + 1) * per_group):
            if q:
                copy_out(q).wait_recv()
        part = pl.ds(g * g_rows, g_rows)
        if g == 0:
            w_copies[0].wait()
            w_copies[1].wait()

        def up(n, _):
            cols = pl.ds(pl.multiple_of(n * 256, 256), 256)
            a = jnp.dot(recv_ref[part, :], wg_ref[:, cols], preferred_element_type=F32)
            b = jnp.dot(recv_ref[part, :], wu_ref[:, cols], preferred_element_type=F32)
            h_ref[:, cols] = (jax.nn.silu(a) * b).astype(BF16)
            return 0

        lax.fori_loop(0, d_ff // 256, up, 0)
        if g == 0:
            w_copies[2].wait()

        def down(n, _):
            cols = pl.ds(pl.multiple_of(n * 256, 256), 256)
            y_ref[part, cols] = jnp.dot(h_ref[...], wd_ref[:, cols], preferred_element_type=F32).astype(BF16)
            return 0

        lax.fori_loop(0, d_model // 256, down, 0)
        for q in range(g * per_group, (g + 1) * per_group):
            if q:
                copy_back(q).start()
    ret_ref[0:cap, :] = y_ref[0:cap, :]

    for g in range(N_GROUPS):
        for q in range(g * per_group, (g + 1) * per_group):
            if q:
                copy_back(q).wait_recv()

        def combine(n, _):
            cols = pl.ds(pl.multiple_of(n * 256, 256), 256)
            routed = jnp.dot(perm_ref[:, g * g_rows:(g + 1) * g_rows], ret_ref[g * g_rows:(g + 1) * g_rows, cols],
                             preferred_element_type=F32)
            total = gcol_ref[:, 0:1] * routed[0:rows]
            for j in range(1, top_k):
                total = total + gcol_ref[:, j:j + 1] * routed[j * rows:(j + 1) * rows]
            out_ref[:, cols] = total if g == 0 else out_ref[:, cols] + total
            return 0

        lax.fori_loop(0, d_model // 256, combine, 0)
    for q in range(1, n_dev):
        copy_out(q).wait_send()
        copy_back(q).wait_send()


def solution(mesh):
    n_outer, n_inner = mesh.shape['ep2'], mesh.shape['ep']
    row_spec = P(('dp', 'ep2', 'ep'), None)
    weight_spec = P(('ep2', 'ep'), None, None)
    order = offsets_in_order(n_outer, n_inner)

    def local_step(tokens, expert_idx, gates, w_gate, w_up, w_down):
        rows, d_model = tokens.shape
        top_k = expert_idx.shape[1]
        d_ff = w_gate.shape[2]
        n_dev = n_outer * n_inner
        n_slots = rows * top_k
        any_spec = pl.BlockSpec(memory_space=pl.ANY)
        dma = pltpu.SemaphoreType.DMA
        mixed = pl.pallas_call(
            functools.partial(layer_kernel, order, n_outer, n_inner),
            out_shape=jax.ShapeDtypeStruct((rows, d_model), F32),
            in_specs=[any_spec] * 6,
            out_specs=pl.BlockSpec(memory_space=pltpu.VMEM),
            scratch_shapes=[
                pltpu.VMEM((top_k, rows), I32),
                pltpu.VMEM((top_k, rows), F32),
                pltpu.VMEM((rows, d_model), BF16),
                pltpu.VMEM((d_model, d_ff), BF16),
                pltpu.VMEM((d_model, d_ff), BF16),
                pltpu.VMEM((d_ff, d_model), BF16),
                pltpu.VMEM((n_dev, rows), F32),
                pltpu.VMEM((n_slots, rows), BF16),
                pltpu.VMEM((n_slots, n_slots), BF16),
                pltpu.VMEM((rows, 8), F32),
                pltpu.VMEM((n_slots, d_model), BF16),
                pltpu.VMEM((n_slots, d_model), BF16),
                pltpu.VMEM((n_slots // N_GROUPS, d_ff), BF16),
                pltpu.VMEM((n_slots, d_model), BF16),
                pltpu.VMEM((n_slots, d_model), BF16),
                dma((3,)), dma((3,)),
                dma((n_dev,)), dma((n_dev,)), dma((n_dev,)), dma((n_dev,)),
            ],
            compiler_params=pltpu.CompilerParams(collective_id=0, has_side_effects=True,
                                                 vmem_limit_bytes=40 * 1024 * 1024),
        )(expert_idx.T, gates.T, tokens, w_gate, w_up, w_down)
        return (tokens.astype(F32) + mixed).astype(BF16)

    return jax.shard_map(local_step, mesh=mesh, in_specs=(row_spec, row_spec, row_spec, weight_spec, weight_spec, weight_spec),
                         out_specs=row_spec, check_vma=False)
```

time: 161 us -> 70.6 us (0.44)
  blocking collectives: 89.1 us -> 0 us
  Pallas kernels: 0 us -> 64 us
  waiting for transfers between devices: 25.7 us -> 0 us
  matrix products: 12.3 us -> 0 us
  other arithmetic: 11.4 us -> 0.9 us
  local copies, waits for them, and re-layouts: 13.9 us -> 5.49 us
  starting transfers between devices: 7.82 us -> 0 us
    all_to_all x3 -> x0, blocking collectives: 89.1 us -> none  [the longest x1 32.2 us: local_step(): received = lax.all_to_all(send_buf, 'ep', 1, 1, tiled=True)]
    pallas_call x0 -> x1, Pallas kernels: none -> 64 us  [local_step(): pl.pallas_call(functools.partial(layer_kernel, order, n_outer, n_inner),...]
    all_to_all x1 -> x0, waiting for transfers between devices: 25.7 us -> none  [local_step(): returned = lax.all_to_all(returned, 'ep', 1, 1, tiled=True)]
    dot_general x3 -> x0, matrix products: 12.3 us -> none  [the longest x1 4.17 us: local_step(): jnp.einsum('abecd,edf->abecf', received, w_up, preferred_element_type=jnp...]
    gather x3 -> x0, local copies, waits for them, and re-layouts: 8.54 us -> none  [the longest x2 6.08 us: local_step(): jnp.take(returned.reshape(n_slots, d_model), slot_ids, axis=0)]
    all_to_all x1 -> x0, starting transfers between devices: 7.82 us -> none  [local_step(): returned = lax.all_to_all(returned, 'ep', 1, 1, tiled=True)]
    unnamed x20 -> x8, local copies, waits for them, and re-layouts: 1.01 us -> 5.49 us
    reduce_sum x2 -> x0, other arithmetic: 4.17 us -> none  [the longest x1 4.07 us: local_step(): mixed = jnp.sum(gates[:, :, None] * routed, axis=1)]
  transfers between devices with their start and end apart: 1 -> 0, of which waited for: 1 -> 0; matrix products, arithmetic and copies ran while one was open for 0% -> 0% of each run, Pallas kernels for 0% -> 0%
where the time goes in v1:
time: 70.6 us; the launch traced here: 70.4 us
  Pallas kernels  64 us (91%)
  local copies, waits for them, and re-layouts  5.49 us (8%)
  other arithmetic  0.9 us (1%)
    pallas_call x1, Pallas kernels, local_step(): pl.pallas_call(functools.partial(layer_kernel, order, n_outer, n_inner),...  64 us
    unnamed x8, local copies, waits for them, and re-layouts  5.49 us

profile of v1, /device:TPU:97, one launch (start us, length us, event | category | flops | bytes accessed | tf_op | source)
XLA Modules:
  0.0 70.4 jit_solution(11389797302682950575)
XLA Ops:
  0.0 0.0 copy-start
  0.0 3.1 %copy-done = bf16[1,2048,1792]{2,1,0:T(8,128)(2,1)S(1)} copy-done((bf16[1,2048,1792]{2,1,0:T(8,128)(2,1)S(1)}, bf16[1,2048,1792]{2,1,0:T(8,128)(2,1)}, u32[]{:S(2)}) %copy-start) | copy-done | bytes 7340056
  3.1 0.0 copy-start.1
  3.1 1.0 %copy-done.1 = bf16[128,2048]{1,0:T(8,128)(2,1)S(1)} copy-done((bf16[128,2048]{1,0:T(8,128)(2,1)S(1)}, bf16[128,2048]{1,0:T(8,128)(2,1)}, u32[]{:S(2)}) %copy-start.1) | copy-done | bytes 524312
  4.1 0.0 copy-start.2
  4.1 0.7 copy-done.2
  4.8 0.0 copy-start.3
  4.8 0.7 copy-done.3
  5.5 64.0 %shard_map.64 = f32[128,2048]{1,0:T(8,128)S(1)} custom-call(s32[4,128]{1,0:T(4,128)S(1)} %bitcast.2, f32[4,128]{1,0:T(4,128)S(1)} %bitcast.3, bf16[128,2048]{1,0:T(8,128)(2,1)S(1)} %copy-done.1, bf16[1,2048,1792]{2,1,0:T(8,128)(2,1)S(1)} %copy-done, bf16[1,2048,1792]{2,1,0:T(8,128)(2,1)} %wu_hbm.1, bf16[1,1792,2048]{2,1,0:T(8,128)(2,1)} %wd_hbm.1), custom_call_target="tpu_custom_call" | custom-call | tf_op jit(solution)/shard_map/pallas_call | solution.py:178
  69.5 0.9 %add_convert_fusion = bf16[128,2048]{1,0:T(8,128)(2,1)} fusion(f32[128,2048]{1,0:T(8,128)S(1)} %shard_map.64, bf16[128,2048]{1,0:T(8,128)(2,1)S(1)} %copy-done.1), kind=kLoop, calls=%fused_computation | loop fusion | flops 786432 | bytes 2097152 | tf_op jit(solution)/shard_map/convert_element_type | solution.py:205
Async XLA Ops:
  0.0 3.1 %copy-start = (bf16[1,2048,1792]{2,1,0:T(8,128)(2,1)S(1)}, bf16[1,2048,1792]{2,1,0:T(8,128)(2,1)}, u32[]{:S(2)}) copy-start(bf16[1,2048,1792]{2,1,0:T(8,128)(2,1)} %wg_hbm.1) | copy-start | bytes 22020100
  3.1 1.0 %copy-start.1 = (bf16[128,2048]{1,0:T(8,128)(2,1)S(1)}, bf16[128,2048]{1,0:T(8,128)(2,1)}, u32[]{:S(2)}) copy-start(bf16[128,2048]{1,0:T(8,128)(2,1)} %tok_hbm.1) | copy-start | bytes 1572868
  4.1 0.7 copy-start.2
  4.8 0.7 copy-start.3

commit v2 on v1

--- a/solution.py
+++ b/solution.py
@@ -58,7 +58,7 @@
     gts_copy = pltpu.make_async_copy(gate_hbm, gts_ref, in_sem.at[2])
     w_copies = [pltpu.make_async_copy(h.at[0], v, w_sem.at[i])
                 for i, (h, v) in enumerate(((wg_hbm, wg_ref), (wu_hbm, wu_ref), (wd_hbm, wd_ref)))]
-    for copy in (idx_copy, tok_copy, gts_copy, *w_copies):
+    for copy in (idx_copy, tok_copy, gts_copy):
         copy.start()
 
     idx_copy.wait()
@@ -75,12 +75,6 @@
         row = slot_ref[pl.ds(y * n_inner + x, 1), :]
         sel_ref[q * cap:(q + 1) * cap, :] = jnp.where(row == place, 1.0, 0.0).astype(BF16)
 
-    tok_copy.wait()
-    for g in range(N_GROUPS):
-        block = sel_ref[g * g_rows:(g + 1) * g_rows, :]
-        send_ref[g * g_rows:(g + 1) * g_rows, :] = jnp.dot(block, tok_ref[...], preferred_element_type=F32).astype(BF16)
-    pl.semaphore_wait(barrier, n_dev - 1)
-
     def copy_out(q):
         y, x = peer(order[q], 1)
         part = pl.ds(q * cap, cap)
@@ -93,12 +87,22 @@
         return pltpu.make_async_remote_copy(y_ref.at[part], ret_ref.at[part], back_send.at[q], back_recv.at[q],
                                             device_id=(dp, y, x), device_id_type=MESH)
 
-    for q in range(1, n_dev):
-        copy_out(q).start()
+    tok_copy.wait()
+    for copy in w_copies:
+        copy.start()
+    for g in range(N_GROUPS):
+        block = sel_ref[g * g_rows:(g + 1) * g_rows, :]
+        send_ref[g * g_rows:(g + 1) * g_rows, :] = jnp.dot(block, tok_ref[...], preferred_element_type=F32).astype(BF16)
+        if g == 0:
+            pl.semaphore_wait(barrier, n_dev - 1)
+        for q in range(max(1, g * per_group), (g + 1) * per_group):
+            copy_out(q).start()
     recv_ref[0:cap, :] = send_ref[0:cap, :]
 
     gts_copy.wait()
-    gcol_ref[...] = jnp.transpose(jnp.concatenate([gts_ref[...], jnp.zeros((8 - top_k, rows), F32)], axis=0))
+    gate_cols = jnp.transpose(jnp.concatenate([gts_ref[...], jnp.zeros((8 - top_k, rows), F32)], axis=0))
+    for j in range(top_k):
+        gcol_ref[j] = jnp.broadcast_to(gate_cols[:, j:j + 1], (rows, 128))
     for g in range(N_GROUPS):
         for j in range(top_k):
             parts = []
@@ -119,22 +123,22 @@
             w_copies[1].wait()
 
         def up(n, _):
-            cols = pl.ds(pl.multiple_of(n * 256, 256), 256)
+            cols = pl.ds(pl.multiple_of(n * 896, 128), 896)
             a = jnp.dot(recv_ref[part, :], wg_ref[:, cols], preferred_element_type=F32)
             b = jnp.dot(recv_ref[part, :], wu_ref[:, cols], preferred_element_type=F32)
             h_ref[:, cols] = (jax.nn.silu(a) * b).astype(BF16)
             return 0
 
-        lax.fori_loop(0, d_ff // 256, up, 0)
+        lax.fori_loop(0, d_ff // 896, up, 0)
         if g == 0:
             w_copies[2].wait()
 
         def down(n, _):
-            cols = pl.ds(pl.multiple_of(n * 256, 256), 256)
+            cols = pl.ds(pl.multiple_of(n * 1024, 256), 1024)
             y_ref[part, cols] = jnp.dot(h_ref[...], wd_ref[:, cols], preferred_element_type=F32).astype(BF16)
             return 0
 
-        lax.fori_loop(0, d_model // 256, down, 0)
+        lax.fori_loop(0, d_model // 1024, down, 0)
         for q in range(g * per_group, (g + 1) * per_group):
             if q:
                 copy_back(q).start()
@@ -146,16 +150,17 @@
                 copy_back(q).wait_recv()
 
         def combine(n, _):
-            cols = pl.ds(pl.multiple_of(n * 256, 256), 256)
+            cols = pl.ds(pl.multiple_of(n * 1024, 1024), 1024)
             routed = jnp.dot(perm_ref[:, g * g_rows:(g + 1) * g_rows], ret_ref[g * g_rows:(g + 1) * g_rows, cols],
                              preferred_element_type=F32)
-            total = gcol_ref[:, 0:1] * routed[0:rows]
+            gate = [jnp.concatenate([gcol_ref[j]] * (1024 // 128), axis=1) for j in range(top_k)]
+            total = gate[0] * routed[0:rows]
             for j in range(1, top_k):
-                total = total + gcol_ref[:, j:j + 1] * routed[j * rows:(j + 1) * rows]
+                total = total + gate[j] * routed[j * rows:(j + 1) * rows]
             out_ref[:, cols] = total if g == 0 else out_ref[:, cols] + total
             return 0
 
-        lax.fori_loop(0, d_model // 256, combine, 0)
+        lax.fori_loop(0, d_model // 1024, combine, 0)
     for q in range(1, n_dev):
         copy_out(q).wait_send()
         copy_back(q).wait_send()
@@ -190,7 +195,7 @@
                 pltpu.VMEM((n_dev, rows), F32),
                 pltpu.VMEM((n_slots, rows), BF16),
                 pltpu.VMEM((n_slots, n_slots), BF16),
-                pltpu.VMEM((rows, 8), F32),
+                pltpu.VMEM((top_k, rows, 128), F32),
                 pltpu.VMEM((n_slots, d_model), BF16),
                 pltpu.VMEM((n_slots, d_model), BF16),
                 pltpu.VMEM((n_slots // N_GROUPS, d_ff), BF16),
@@ -201,7 +206,8 @@
             ],
             compiler_params=pltpu.CompilerParams(collective_id=0, has_side_effects=True,
                                                  vmem_limit_bytes=40 * 1024 * 1024),
-        )(expert_idx.T, gates.T, tokens, w_gate, w_up, w_down)
+        )(*[pltpu.with_memory_space_constraint(v, pltpu.HBM)
+            for v in (expert_idx.T, gates.T, tokens, w_gate, w_up, w_down)])
         return (tokens.astype(F32) + mixed).astype(BF16)
 
     return jax.shard_map(local_step, mesh=mesh, in_specs=(row_spec, row_spec, row_spec, weight_spec, weight_spec, weight_spec),

time: 70.6 us -> 61.7 us (0.87)
  local copies, waits for them, and re-layouts: 5.49 us -> 0.01 us
  Pallas kernels: 64 us -> 60.7 us
    unnamed x8 -> x2, local copies, waits for them, and re-layouts: 5.49 us -> 0.01 us
    pallas_call x1, Pallas kernels: 64 us -> 60.7 us  [local_step(): pl.pallas_call(functools.partial(layer_kernel, order, n_outer, n_inner),...]
where the time goes in v2:
time: 61.7 us
  Pallas kernels  60.7 us (98%)
  other arithmetic  0.9 us (1%)
    pallas_call x1, Pallas kernels, local_step(): pl.pallas_call(functools.partial(layer_kernel, order, n_outer, n_inner),...  60.7 us

profile of v2, /device:TPU:97, one launch (start us, length us, event | category | flops | bytes accessed | tf_op | source)
XLA Modules:
  0.0 61.7 jit_solution(8833857009656867192)
XLA Ops:
  0.0 0.0 copy-start
  0.0 60.7 %shard_map.64 = f32[128,2048]{1,0:T(8,128)S(1)} custom-call(s32[4,128]{1,0:T(4,128)} %bitcast.2, f32[4,128]{1,0:T(4,128)} %bitcast.3, bf16[128,2048]{1,0:T(8,128)(2,1)} %tok_hbm.1, bf16[1,2048,1792]{2,1,0:T(8,128)(2,1)} %wg_hbm.1, bf16[1,2048,1792]{2,1,0:T(8,128)(2,1)} %wu_hbm.1, bf16[1,1792,2048]{2,1,0:T(8,128)(2,1)} %wd_hbm.1), custom_call_target="tpu_custom_call" | custom-call | tf_op jit(solution)/shard_map/pallas_call | solution.py:183
  60.7 0.0 copy-done
  60.7 0.9 %add_convert_fusion = bf16[128,2048]{1,0:T(8,128)(2,1)} fusion(f32[128,2048]{1,0:T(8,128)S(1)} %shard_map.64, bf16[128,2048]{1,0:T(8,128)(2,1)S(1)} %copy-done), kind=kLoop, calls=%fused_computation | loop fusion | flops 786432 | bytes 2097152 | tf_op jit(solution)/shard_map/convert_element_type | solution.py:211
Async XLA Ops:
  0.0 60.7 %copy-start = (bf16[128,2048]{1,0:T(8,128)(2,1)S(1)}, bf16[128,2048]{1,0:T(8,128)(2,1)}, u32[]{:S(2)}) copy-start(bf16[128,2048]{1,0:T(8,128)(2,1)} %tok_hbm.1) | copy-start | bytes 1572868

commit v3 on v0

v3 whole, which is shorter than its diff:
```python
import functools

import jax
import jax.numpy as jnp
from jax import lax
from jax.experimental import pallas as pl
from jax.experimental.pallas import tpu as pltpu
from jax.sharding import PartitionSpec as P

MESH = pl.DeviceIdType.MESH
BF16, F32, I32 = jnp.bfloat16, jnp.float32, jnp.int32
RING = 4
CLOSE = (0, 1, 3)
GROUPS = []
for _dc in (0, 1):
    GROUPS.append([(dx, dy, _dc) for dy in CLOSE for dx in CLOSE][:8])
    GROUPS.append([(3, 3, _dc)] + [(dx, dy, _dc) for dy in range(RING) for dx in range(RING) if 2 in (dx, dy)])
ORDER = sum(GROUPS, [])
SLOT = {o: q for q, o in enumerate(ORDER)}
FIRST = [sum(len(g) for g in GROUPS[:i]) for i in range(len(GROUPS) + 1)]


def layer_kernel(idx_hbm, gate_hbm, tok_hbm, wg_hbm, wu_hbm, wd_hbm, out_ref,
                 idx_ref, gts_ref, tok_ref, near_ref, wg_ref, wu_ref, wd_ref, tab_ref, perm_ref, gcol_ref,
                 gath_ref, recv_ref, x_ref, h_ref, y_ref, ret_ref,
                 in_sem, w_sem, tab_send, tab_recv, own_send, own_recv, relay_send, relay_recv,
                 out_send, out_recv, back_send, back_recv):
    dp, outer, inner = lax.axis_index('dp'), lax.axis_index('ep2'), lax.axis_index('ep')
    chip, core = inner // 2, inner % 2
    top_k, rows = idx_ref.shape
    n_dev = len(ORDER)
    cap = (rows * top_k) // n_dev
    d_model, d_ff = wg_ref.shape
    half = d_model // 2

    def place(dx, dy, dc, sign=1):
        y = lax.rem(outer + (dy if sign > 0 else RING - dy), RING)
        x = lax.rem(chip + (dx if sign > 0 else RING - dx), RING)
        return y, x * 2 + lax.rem(core + dc, 2)

    def expert(dx, dy, dc):
        y, x = place(dx, dy, dc)
        return y * (2 * RING) + x

    def remote(src, dst, send, recv, where):
        return pltpu.make_async_remote_copy(src, dst, send, recv, device_id=(dp, *where), device_id_type=MESH)

    def along(axis, k):
        return place(k, 0, 0) if axis == 0 else place(0, k, 0)

    barrier = pltpu.get_barrier_semaphore()
    for o in ORDER[1:]:
        pl.semaphore_signal(barrier, inc=1, device_id=(dp, *place(*o)), device_id_type=MESH)

    idx_copy = pltpu.make_async_copy(idx_hbm, idx_ref, in_sem.at[0])
    gts_copy = pltpu.make_async_copy(gate_hbm, gts_ref, in_sem.at[1])
    tok_copies = [pltpu.make_async_copy(tok_hbm.at[:, pl.ds(a * half, half)], tok_ref.at[a], in_sem.at[2 + a])
                  for a in (0, 1)]
    w_copies = [pltpu.make_async_copy(h.at[0], v, w_sem.at[i])
                for i, (h, v) in enumerate(((wg_hbm, wg_ref), (wu_hbm, wu_ref), (wd_hbm, wd_ref)))]
    for copy in (idx_copy, *tok_copies, gts_copy):
        copy.start()

    idx_copy.wait()
    ids = lax.broadcasted_iota(I32, (n_dev, rows), 0)
    chosen = jnp.zeros((n_dev, rows), F32)
    for j in range(top_k):
        chosen = chosen + jnp.where(idx_ref[j:j + 1, :] == ids, 1.0, 0.0)
    earlier = lax.broadcasted_iota(I32, (rows, rows), 0) < lax.broadcasted_iota(I32, (rows, rows), 1)
    rank = jnp.dot(chosen.astype(BF16), jnp.where(earlier, 1.0, 0.0).astype(BF16), preferred_element_type=F32)
    table = jnp.where(chosen > 0.5, rank, -1.0)
    tab_ref[0, 0] = table
    tab_ref[1, 0] = table

    started = []

    def go(copies):
        for copy in copies:
            copy.start()
            started.append(copy)

    def own(a, k):
        return remote(tok_ref.at[a], near_ref.at[a, k - 1], own_send.at[a, k // 2], own_recv.at[a, k // 2], along(a, k))

    def relay(a, k):
        part = pl.ds((k // 2) * (rows // 2), rows // 2)
        return remote(near_ref.at[a, k - 1, part], near_ref.at[a, 1, part],
                      relay_send.at[a, k // 2], relay_recv.at[a, k // 2], along(a, k))

    def table_to(a, k):
        return remote(tab_ref.at[a, 0], tab_ref.at[a, k], tab_send.at[a, k - 1], tab_recv.at[a, k - 1], along(a, k))

    def block(a, i, d, dc):
        q = SLOT[(i, d, dc) if a == 0 else (d, i, dc)]
        return remote(gath_ref.at[a, i, pl.ds((dc * RING + d) * cap, cap)], recv_ref.at[a, pl.ds(q * cap, cap)],
                      out_send.at[a, q], out_recv.at[a, q], place(0, d, dc) if a == 0 else place(d, 0, dc))

    def blocks(i, dc):
        return [block(a, i, d, dc) for d in (2, 1, 3, 0) for a in (0, 1) if d or dc]

    rank_of = lax.broadcasted_iota(I32, (cap, rows), 0).astype(F32)

    def picks(a, i, e):
        return jnp.where(tab_ref[a, i, pl.ds(e, 1), :] == rank_of, 1.0, 0.0).astype(BF16)

    def gather(a, i):
        picked = jnp.concatenate(
            [picks(a, i, expert(0, d, dc) if a == 0 else expert(d, 0, dc)) for dc in (0, 1) for d in range(RING)], axis=0)
        source = tok_ref[a] if i == 0 else near_ref[a, i - 1]
        gath_ref[a, i] = jnp.dot(picked, source, preferred_element_type=F32).astype(BF16)

    for copy in tok_copies:
        copy.wait()
    pl.semaphore_wait(barrier, n_dev - 1)
    go([own(a, k) for a in (0, 1) for k in (1, 3)])
    go([table_to(a, k) for k in (2, 1, 3) for a in (0, 1)])
    for copy in w_copies:
        copy.start()
    gather(0, 0)
    gather(1, 0)
    go(blocks(0, 0))
    for k in (1, 3):
        for a in (0, 1):
            own(a, k).wait_recv()
            go([relay(a, k)])
    for k in (1, 3, 2):
        for a in (0, 1):
            table_to(a, k).wait_recv()
    for k in (1, 3):
        for a in (0, 1):
            gather(a, k)
        go(blocks(k, 0))
    go(blocks(0, 1))
    for k in (1, 3):
        for a in (0, 1):
            relay(a, k).wait_recv()
    for a in (0, 1):
        gather(a, 2)
    go(blocks(2, 0) + blocks(1, 1) + blocks(3, 1) + blocks(2, 1))
    for i in range(RING):
        for a in (0, 1):
            q = SLOT[(i, 0, 0) if a == 0 else (0, i, 0)]
            recv_ref[a, q * cap:(q + 1) * cap, :] = gath_ref[a, i, 0:cap, :]

    gts_copy.wait()
    gate_cols = jnp.transpose(jnp.concatenate([gts_ref[...], jnp.zeros((8 - top_k, rows), F32)], axis=0))
    for j in range(top_k):
        gcol_ref[j] = jnp.broadcast_to(gate_cols[:, j:j + 1], (rows, 128))
    per = 128 // cap
    for g in range(n_dev // per):
        for j in range(top_k):
            parts = []
            for q in range(g * per, (g + 1) * per):
                e = expert(*ORDER[q])
                mine = jnp.where(idx_ref[j:j + 1, :] == e, 1.0, 0.0)
                parts.append(jnp.where(tab_ref[0, 0, pl.ds(e, 1), :] == rank_of, 1.0, 0.0) * mine)
            perm_ref[j * rows:(j + 1) * rows, g * 128:(g + 1) * 128] = jnp.transpose(
                jnp.concatenate(parts, axis=0)).astype(BF16)

    def back(o):
        part = pl.ds(SLOT[o] * cap, cap)
        return remote(y_ref.at[part], ret_ref.at[part], back_send.at[SLOT[o]], back_recv.at[SLOT[o]], place(*o, -1))

    def hops(o):
        return sum(min(d, RING - d) for d in o[:2])

    for g, group in enumerate(GROUPS):
        for dx, dy, dc in group:
            if dy or dc:
                block(0, dx, dy, dc).wait_recv()
            if dx or dc:
                block(1, dy, dx, dc).wait_recv()
        n = len(group) * cap
        part = pl.ds(FIRST[g] * cap, n)
        x_ref[0:n, 0:half] = recv_ref[0, part, :]
        x_ref[0:n, half:] = recv_ref[1, part, :]
        if g == 0:
            w_copies[0].wait()
            w_copies[1].wait()

        def up(m, _):
            cols = pl.ds(pl.multiple_of(m * (d_ff // 2), 128), d_ff // 2)
            a = jnp.dot(x_ref[0:n, :], wg_ref[:, cols], preferred_element_type=F32)
            b = jnp.dot(x_ref[0:n, :], wu_ref[:, cols], preferred_element_type=F32)
            h_ref[0:n, cols] = (jax.nn.silu(a) * b).astype(BF16)
            return 0

        lax.fori_loop(0, 2, up, 0)
        if g == 0:
            w_copies[2].wait()

        def down(m, _):
            cols = pl.ds(pl.multiple_of(m * half, half), half)
            y_ref[part, cols] = jnp.dot(h_ref[0:n, :], wd_ref[:, cols], preferred_element_type=F32).astype(BF16)
            return 0

        lax.fori_loop(0, 2, down, 0)
        for o in group:
            if any(o):
                copy = back(o)
                copy.start()
                started.append(copy)
    own_part = pl.ds(0, cap)
    ret_ref[own_part, :] = y_ref[own_part, :]

    span = n_dev * cap // 2
    for g in (0, 1):
        for o in GROUPS[2 * g] + GROUPS[2 * g + 1]:
            if any(o):
                back(o).wait_recv()
        part = pl.ds(g * span, span)

        def combine(m, _):
            cols = pl.ds(pl.multiple_of(m * half, half), half)
            routed = jnp.dot(perm_ref[:, g * span:(g + 1) * span], ret_ref[part, cols], preferred_element_type=F32)
            total = None
            for j in range(top_k):
                gate = jnp.concatenate([gcol_ref[j]] * (half // 128), axis=1)
                term = gate * routed[j * rows:(j + 1) * rows]
                total = term if j == 0 else total + term
            out_ref[:, cols] = total if g == 0 else out_ref[:, cols] + total
            return 0

        lax.fori_loop(0, 2, combine, 0)
    for copy in started:
        copy.wait_send()


def solution(mesh):
    assert mesh.shape['ep2'] == RING and mesh.shape['ep'] == 2 * RING
    row_spec = P(('dp', 'ep2', 'ep'), None)
    weight_spec = P(('ep2', 'ep'), None, None)

    def local_step(tokens, expert_idx, gates, w_gate, w_up, w_down):
        rows, d_model = tokens.shape
        top_k = expert_idx.shape[1]
        d_ff = w_gate.shape[2]
        n_dev = len(ORDER)
        n_slots = rows * top_k
        cap = n_slots // n_dev
        half = d_model // 2
        most = max(len(g) for g in GROUPS) * cap
        dma = pltpu.SemaphoreType.DMA
        mixed = pl.pallas_call(
            layer_kernel,
            out_shape=jax.ShapeDtypeStruct((rows, d_model), F32),
            in_specs=[pl.BlockSpec(memory_space=pl.ANY)] * 6,
            out_specs=pl.BlockSpec(memory_space=pltpu.VMEM),
            scratch_shapes=[
                pltpu.VMEM((top_k, rows), I32),
                pltpu.VMEM((top_k, rows), F32),
                pltpu.VMEM((2, rows, half), BF16),
                pltpu.VMEM((2, RING - 1, rows, half), BF16),
                pltpu.VMEM((d_model, d_ff), BF16),
                pltpu.VMEM((d_model, d_ff), BF16),
                pltpu.VMEM((d_ff, d_model), BF16),
                pltpu.VMEM((2, RING, n_dev, rows), F32),
                pltpu.VMEM((n_slots, n_slots), BF16),
                pltpu.VMEM((top_k, rows, 128), F32),
                pltpu.VMEM((2, RING, 2 * RING * cap, half), BF16),
                pltpu.VMEM((2, n_slots, half), BF16),
                pltpu.VMEM((most, d_model), BF16),
                pltpu.VMEM((most, d_ff), BF16),
                pltpu.VMEM((n_slots, d_model), BF16),
                pltpu.VMEM((n_slots, d_model), BF16),
                dma((4,)), dma((3,)), dma((2, 3)), dma((2, 3)), dma((2, 2)), dma((2, 2)), dma((2, 2)), dma((2, 2)),
                dma((2, n_dev)), dma((2, n_dev)), dma((n_dev,)), dma((n_dev,)),
            ],
            compiler_params=pltpu.CompilerParams(collective_id=0, has_side_effects=True,
                                                 vmem_limit_bytes=44 * 1024 * 1024),
        )(*[pltpu.with_memory_space_constraint(v, pltpu.HBM)
            for v in (expert_idx.T, gates.T, tokens, w_gate, w_up, w_down)])
        return (tokens.astype(F32) + mixed).astype(BF16)

    return jax.shard_map(local_step, mesh=mesh, in_specs=(row_spec, row_spec, row_spec, weight_spec, weight_spec, weight_spec),
                         out_specs=row_spec, check_vma=False)
```

time: 161 us -> 59.9 us (0.37)
  blocking collectives: 89.1 us -> 0 us
  Pallas kernels: 0 us -> 58.9 us
  waiting for transfers between devices: 25.7 us -> 0 us
  local copies, waits for them, and re-layouts: 13.9 us -> 0.01 us
  matrix products: 12.3 us -> 0 us
  other arithmetic: 11.4 us -> 0.9 us
  starting transfers between devices: 7.82 us -> 0 us
    all_to_all x3 -> x0, blocking collectives: 89.1 us -> none  [the longest x1 32.2 us: local_step(): received = lax.all_to_all(send_buf, 'ep', 1, 1, tiled=True)]
    pallas_call x0 -> x1, Pallas kernels: none -> 58.9 us  [local_step(): pl.pallas_call(layer_kernel, out_shape=jax.ShapeDtypeStruct((rows, d_mode...]
    all_to_all x1 -> x0, waiting for transfers between devices: 25.7 us -> none  [local_step(): returned = lax.all_to_all(returned, 'ep', 1, 1, tiled=True)]
    dot_general x3 -> x0, matrix products: 12.3 us -> none  [the longest x1 4.17 us: local_step(): jnp.einsum('abecd,edf->abecf', received, w_up, preferred_element_type=jnp...]
    gather x3 -> x0, local copies, waits for them, and re-layouts: 8.54 us -> none  [the longest x2 6.08 us: local_step(): jnp.take(returned.reshape(n_slots, d_model), slot_ids, axis=0)]
    all_to_all x1 -> x0, starting transfers between devices: 7.82 us -> none  [local_step(): returned = lax.all_to_all(returned, 'ep', 1, 1, tiled=True)]
    reduce_sum x2 -> x0, other arithmetic: 4.17 us -> none  [the longest x1 4.07 us: local_step(): mixed = jnp.sum(gates[:, :, None] * routed, axis=1)]
    scatter-add x1 -> x0, other arithmetic: 4.09 us -> none  [local_step(): jax.ops.segment_sum(token_of - tok_rows, slot_ids, num_segments=n_slots)]
  transfers between devices with their start and end apart: 1 -> 0, of which waited for: 1 -> 0; matrix products, arithmetic and copies ran while one was open for 0% -> 0% of each run, Pallas kernels for 0% -> 0%
where the time goes in v3:
time: 59.9 us; the launch traced here: 59.8 us
  Pallas kernels  58.9 us (98%)
  other arithmetic  0.9 us (2%)
    pallas_call x1, Pallas kernels, local_step(): pl.pallas_call(layer_kernel, out_shape=jax.ShapeDtypeStruct((rows, d_mode...  58.9 us

profile of v3, /device:TPU:97, one launch (start us, length us, event | category | flops | bytes accessed | tf_op | source)
XLA Modules:
  0.0 59.8 jit_solution(15642326598299444200)
XLA Ops:
  0.0 0.0 copy-start
  0.0 58.9 %shard_map.64 = f32[128,2048]{1,0:T(8,128)S(1)} custom-call(s32[4,128]{1,0:T(4,128)} %bitcast.2, f32[4,128]{1,0:T(4,128)} %bitcast.3, bf16[128,2048]{1,0:T(8,128)(2,1)} %tok_hbm.1, bf16[1,2048,1792]{2,1,0:T(8,128)(2,1)} %wg_hbm.1, bf16[1,2048,1792]{2,1,0:T(8,128)(2,1)} %wu_hbm.1, bf16[1,1792,2048]{2,1,0:T(8,128)(2,1)} %wd_hbm.1), custom_call_target="tpu_custom_call" | custom-call | tf_op jit(solution)/shard_map/pallas_call | solution.py:244
  58.9 0.0 copy-done
  58.9 0.9 %add_convert_fusion = bf16[128,2048]{1,0:T(8,128)(2,1)} fusion(f32[128,2048]{1,0:T(8,128)S(1)} %shard_map.64, bf16[128,2048]{1,0:T(8,128)(2,1)S(1)} %copy-done), kind=kLoop, calls=%fused_computation | loop fusion | flops 786432 | bytes 2097152 | tf_op jit(solution)/shard_map/convert_element_type | solution.py:273
Async XLA Ops:
  0.0 58.9 %copy-start = (bf16[128,2048]{1,0:T(8,128)(2,1)S(1)}, bf16[128,2048]{1,0:T(8,128)(2,1)}, u32[]{:S(2)}) copy-start(bf16[128,2048]{1,0:T(8,128)(2,1)} %tok_hbm.1) | copy-start | bytes 1572868

commit v4 on v3

--- a/solution.py
+++ b/solution.py
@@ -96,7 +96,7 @@
                       out_send.at[a, q], out_recv.at[a, q], place(0, d, dc) if a == 0 else place(d, 0, dc))
 
     def blocks(i, dc):
-        return [block(a, i, d, dc) for d in (2, 1, 3, 0) for a in (0, 1) if d or dc]
+        return [block(a, i, d, dc) for d in (0, 1, 3, 2) for a in (0, 1) if d or dc]
 
     rank_of = lax.broadcasted_iota(I32, (cap, rows), 0).astype(F32)
 
@@ -195,11 +195,14 @@
             return 0
 
         lax.fori_loop(0, 2, down, 0)
-        for o in group:
+        for o in sorted(group, key=lambda o: -hops(o)) if g == 3 else group:
             if any(o):
                 copy = back(o)
                 copy.start()
                 started.append(copy)
+    early = len(started) - len(GROUPS[-1]) - len(GROUPS[-2])
+    for copy in started[:early]:
+        copy.wait_send()
     own_part = pl.ds(0, cap)
     ret_ref[own_part, :] = y_ref[own_part, :]
 
@@ -222,7 +225,7 @@
             return 0
 
         lax.fori_loop(0, 2, combine, 0)
-    for copy in started:
+    for copy in started[early:]:
         copy.wait_send()
 
 

time: 59.9 us -> 59.1 us (0.987)
  Pallas kernels: 58.9 us -> 58 us
    pallas_call x1, Pallas kernels: 58.9 us -> 58 us  [local_step(): pl.pallas_call(layer_kernel, out_shape=jax.ShapeDtypeStruct((rows, d_mode...]
where the time goes in v4:
time: 59.1 us; the launch traced here: 59 us
  Pallas kernels  58 us (98%)
  other arithmetic  0.9 us (2%)
    pallas_call x1, Pallas kernels, local_step(): pl.pallas_call(layer_kernel, out_shape=jax.ShapeDtypeStruct((rows, d_mode...  58 us

profile of v4, /device:TPU:97, one launch (start us, length us, event | category | flops | bytes accessed | tf_op | source)
XLA Modules:
  0.0 59.0 jit_solution(177632657938190304)
XLA Ops:
  0.0 0.0 copy-start
  0.0 58.0 %shard_map.64 = f32[128,2048]{1,0:T(8,128)S(1)} custom-call(s32[4,128]{1,0:T(4,128)} %bitcast.2, f32[4,128]{1,0:T(4,128)} %bitcast.3, bf16[128,2048]{1,0:T(8,128)(2,1)} %tok_hbm.1, bf16[1,2048,1792]{2,1,0:T(8,128)(2,1)} %wg_hbm.1, bf16[1,2048,1792]{2,1,0:T(8,128)(2,1)} %wu_hbm.1, bf16[1,1792,2048]{2,1,0:T(8,128)(2,1)} %wd_hbm.1), custom_call_target="tpu_custom_call" | custom-call | tf_op jit(solution)/shard_map/pallas_call | solution.py:247
  58.1 0.0 copy-done
  58.1 0.9 %add_convert_fusion = bf16[128,2048]{1,0:T(8,128)(2,1)} fusion(f32[128,2048]{1,0:T(8,128)S(1)} %shard_map.64, bf16[128,2048]{1,0:T(8,128)(2,1)S(1)} %copy-done), kind=kLoop, calls=%fused_computation | loop fusion | flops 786432 | bytes 2097152 | tf_op jit(solution)/shard_map/convert_element_type | solution.py:276
Async XLA Ops:
  0.0 58.1 %copy-start = (bf16[128,2048]{1,0:T(8,128)(2,1)S(1)}, bf16[128,2048]{1,0:T(8,128)(2,1)}, u32[]{:S(2)}) copy-start(bf16[128,2048]{1,0:T(8,128)(2,1)} %tok_hbm.1) | copy-start | bytes 1572868

commit v5 on v4

--- a/solution.py
+++ b/solution.py
@@ -58,8 +58,50 @@
                   for a in (0, 1)]
     w_copies = [pltpu.make_async_copy(h.at[0], v, w_sem.at[i])
                 for i, (h, v) in enumerate(((wg_hbm, wg_ref), (wu_hbm, wu_ref), (wd_hbm, wd_ref)))]
-    for copy in (idx_copy, *tok_copies, gts_copy):
+    for copy in (*tok_copies, idx_copy, gts_copy):
         copy.start()
+
+    started = []
+
+    def go(copies):
+        for copy in copies:
+            copy.start()
+            started.append(copy)
+
+    def own(a, k):
+        return remote(tok_ref.at[a], near_ref.at[a, k - 1], own_send.at[a, k // 2], own_recv.at[a, k // 2], along(a, k))
+
+    def relay(a, k):
+        part = pl.ds((k // 2) * (rows // 2), rows // 2)
+        return remote(near_ref.at[a, k - 1, part], near_ref.at[a, 1, part],
+                      relay_send.at[a, k // 2], relay_recv.at[a, k // 2], along(a, k))
+
+    def table_to(a, k):
+        return remote(tab_ref.at[a, 0], tab_ref.at[a, k], tab_send.at[a, k - 1], tab_recv.at[a, k - 1], along(a, k))
+
+    def block(a, i, d, dc):
+        q = SLOT[(i, d, dc) if a == 0 else (d, i, dc)]
+        return remote(gath_ref.at[a, i, pl.ds((dc * RING + d) * cap, cap)], recv_ref.at[a, pl.ds(q * cap, cap)],
+                      out_send.at[a, q], out_recv.at[a, q], place(0, d, dc) if a == 0 else place(d, 0, dc))
+
+    def blocks(i, dc):
+        return [block(a, i, d, dc) for d in (0, 1, 3, 2) for a in (0, 1) if d or dc]
+
+    rank_of = lax.broadcasted_iota(I32, (cap, rows), 0).astype(F32)
+
+    def picks(a, i, e):
+        return jnp.where(tab_ref[a, i, pl.ds(e, 1), :] == rank_of, 1.0, 0.0).astype(BF16)
+
+    def gather(a, i):
+        picked = jnp.concatenate(
+            [picks(a, i, expert(0, d, dc) if a == 0 else expert(d, 0, dc)) for dc in (0, 1) for d in range(RING)], axis=0)
+        source = tok_ref[a] if i == 0 else near_ref[a, i - 1]
+        gath_ref[a, i] = jnp.dot(picked, source, preferred_element_type=F32).astype(BF16)
+
+    for copy in tok_copies:
+        copy.wait()
+    pl.semaphore_wait(barrier, n_dev - 1)
+    go([own(a, k) for a in (0, 1) for k in (1, 3)])
 
     idx_copy.wait()
     ids = lax.broadcasted_iota(I32, (n_dev, rows), 0)
@@ -72,47 +114,6 @@
     tab_ref[0, 0] = table
     tab_ref[1, 0] = table
 
-    started = []
-
-    def go(copies):
-        for copy in copies:
-            copy.start()
-            started.append(copy)
-
-    def own(a, k):
-        return remote(tok_ref.at[a], near_ref.at[a, k - 1], own_send.at[a, k // 2], own_recv.at[a, k // 2], along(a, k))
-
-    def relay(a, k):
-        part = pl.ds((k // 2) * (rows // 2), rows // 2)
-        return remote(near_ref.at[a, k - 1, part], near_ref.at[a, 1, part],
-                      relay_send.at[a, k // 2], relay_recv.at[a, k // 2], along(a, k))
-
-    def table_to(a, k):
-        return remote(tab_ref.at[a, 0], tab_ref.at[a, k], tab_send.at[a, k - 1], tab_recv.at[a, k - 1], along(a, k))
-
-    def block(a, i, d, dc):
-        q = SLOT[(i, d, dc) if a == 0 else (d, i, dc)]
-        return remote(gath_ref.at[a, i, pl.ds((dc * RING + d) * cap, cap)], recv_ref.at[a, pl.ds(q * cap, cap)],
-                      out_send.at[a, q], out_recv.at[a, q], place(0, d, dc) if a == 0 else place(d, 0, dc))
-
-    def blocks(i, dc):
-        return [block(a, i, d, dc) for d in (0, 1, 3, 2) for a in (0, 1) if d or dc]
-
-    rank_of = lax.broadcasted_iota(I32, (cap, rows), 0).astype(F32)
-
-    def picks(a, i, e):
-        return jnp.where(tab_ref[a, i, pl.ds(e, 1), :] == rank_of, 1.0, 0.0).astype(BF16)
-
-    def gather(a, i):
-        picked = jnp.concatenate(
-            [picks(a, i, expert(0, d, dc) if a == 0 else expert(d, 0, dc)) for dc in (0, 1) for d in range(RING)], axis=0)
-        source = tok_ref[a] if i == 0 else near_ref[a, i - 1]
-        gath_ref[a, i] = jnp.dot(picked, source, preferred_element_type=F32).astype(BF16)
-
-    for copy in tok_copies:
-        copy.wait()
-    pl.semaphore_wait(barrier, n_dev - 1)
-    go([own(a, k) for a in (0, 1) for k in (1, 3)])
     go([table_to(a, k) for k in (2, 1, 3) for a in (0, 1)])
     for copy in w_copies:
         copy.start()

time: 59.1 us -> 59 us (level)
  no operation moved by 1% of the time
where the time goes in v5:
time: 59 us; the launch traced here: 58.9 us
  Pallas kernels  58 us (98%)
  other arithmetic  0.9 us (2%)
    pallas_call x1, Pallas kernels, local_step(): pl.pallas_call(layer_kernel, out_shape=jax.ShapeDtypeStruct((rows, d_mode...  58 us

profile of v5, /device:TPU:97, one launch (start us, length us, event | category | flops | bytes accessed | tf_op | source)
XLA Modules:
  0.0 58.9 jit_solution(894816158268322054)
XLA Ops:
  0.0 0.0 copy-start
  0.0 58.0 %shard_map.64 = f32[128,2048]{1,0:T(8,128)S(1)} custom-call(s32[4,128]{1,0:T(4,128)} %bitcast.2, f32[4,128]{1,0:T(4,128)} %bitcast.3, bf16[128,2048]{1,0:T(8,128)(2,1)} %tok_hbm.1, bf16[1,2048,1792]{2,1,0:T(8,128)(2,1)} %wg_hbm.1, bf16[1,2048,1792]{2,1,0:T(8,128)(2,1)} %wu_hbm.1, bf16[1,1792,2048]{2,1,0:T(8,128)(2,1)} %wd_hbm.1), custom_call_target="tpu_custom_call" | custom-call | tf_op jit(solution)/shard_map/pallas_call | solution.py:248
  58.0 0.0 copy-done
  58.0 0.9 %add_convert_fusion = bf16[128,2048]{1,0:T(8,128)(2,1)} fusion(f32[128,2048]{1,0:T(8,128)S(1)} %shard_map.64, bf16[128,2048]{1,0:T(8,128)(2,1)S(1)} %copy-done), kind=kLoop, calls=%fused_computation | loop fusion | flops 786432 | bytes 2097152 | tf_op jit(solution)/shard_map/convert_element_type | solution.py:277
Async XLA Ops:
  0.0 58.0 %copy-start = (bf16[128,2048]{1,0:T(8,128)(2,1)S(1)}, bf16[128,2048]{1,0:T(8,128)(2,1)}, u32[]{:S(2)}) copy-start(bf16[128,2048]{1,0:T(8,128)(2,1)} %tok_hbm.1) | copy-start | bytes 1572868
